TPU v7x, 128 devices: a whole 4x4x4 slice. The times are simulated.
128 devices in a mesh: pp: 64 (over z, y, x), tp: 2 (over core).
Axes of the slice: x: 4, y: 4, z: 4, core: 2. Of those that a mesh axis runs over, the one named last changes fastest.
Arguments:
- activations: bfloat16 [512, 14, 14, 2560], P(('pp', 'tp'))
- conv_w: bfloat16 [3, 3, 2560, 2560], P(None, None, 'tp')
- bn_scale: float32 [2560], P('tp')
- bn_shift: float32 [2560], P('tp')
Outputs:
- output: bfloat16 [512, 14, 14, 2560], P('pp', None, None, 'tp')
All inputs are finite; a program needn't handle non-finite values.
Results may differ from a plain program's by a relative error of at most 0.001.
Values are sent between devices in bfloat16 or wider.
A program may use at most 1 GiB of HBM per device.

v0:
```python
import functools

import jax
import jax.numpy as jnp
from jax import lax
from jax.experimental import pallas as pl
from jax.experimental.pallas import tpu as pltpu
from jax.sharding import PartitionSpec as P

MESH = pl.DeviceIdType.MESH
TILE = 256
X_ROWS = ((0, 8), (8, 14))
OUT_ROWS = ((0, 6), (6, 14))
VMEM_LIMIT = 67043328


def conv_kernel(half, x, w, scale, shift, zb, za, xr, xs, wbuf, ps0, ps1, pr0, pr1, pown, zbuf,
                xsend, xrecv, xloc, wsem, psend, precv, zsend, zrecv, zloc):
    pp, tp = lax.axis_index("pp"), lax.axis_index("tp")
    on_s1 = pp >= half
    on_s0 = jnp.logical_not(on_s1)
    other_pp = jnp.where(on_s1, pp - half, pp + half)
    peer = 1 - tp
    sends_b = jnp.logical_and(on_s0, tp == 0)
    keeps_a = jnp.logical_and(on_s0, tp == 1)
    hh, ww, nn, cc = x.shape
    ch = cc // 2
    row = ww * nn
    nj = ch // TILE
    ps, pr = (ps0, ps1), (pr0, pr1)

    def w_copies(j, slot):
        for k, blk in enumerate((tp, peer)):
            cols = pl.ds(pl.multiple_of(blk * ch + j * TILE, TILE), TILE)
            yield pltpu.make_async_copy(w.at[:, :, cols], wbuf.at[slot, :, :, pl.ds(k * TILE, TILE)], wsem.at[slot, k])

    def x_send(c, blk, dst):
        lo, hi = X_ROWS[c]
        return pltpu.make_async_remote_copy(
            src_ref=x.at[pl.ds(lo, hi - lo), :, :, pl.ds(blk * ch, ch)],
            dst_ref=xr.at[pl.ds(lo, hi - lo)],
            send_sem=xsend.at[c, blk], recv_sem=xrecv.at[c],
            device_id=dst, device_id_type=MESH)

    def x_keep(c):
        lo, hi = X_ROWS[c]
        return pltpu.make_async_copy(x.at[pl.ds(lo, hi - lo), :, :, pl.ds(ch, ch)], xr.at[pl.ds(lo, hi - lo)], xloc.at[c])

    def p_send(s, j):
        return pltpu.make_async_remote_copy(
            src_ref=ps[s].at[j], dst_ref=pr[s].at[j], send_sem=psend.at[s, j], recv_sem=precv.at[s, j],
            device_id=(pp, peer), device_id_type=MESH)

    def z_rows(s):
        lo, hi = OUT_ROWS[s]
        return pl.ds(lo * row, (hi - lo) * row)

    def z_send(s, j):
        return pltpu.make_async_remote_copy(
            src_ref=zbuf.at[j, z_rows(s)], dst_ref=za.at[j, z_rows(s)], send_sem=zsend.at[s, j], recv_sem=zrecv.at[s, j],
            device_id=(other_pp, tp), device_id_type=MESH)

    def z_keep(s, j):
        return pltpu.make_async_copy(zbuf.at[j, z_rows(s)], zb.at[j, z_rows(s)], zloc.at[s, j])

    for copy in w_copies(0, 0):
        copy.start()

    @pl.when(keeps_a)
    def _():
        for c in range(2):
            x_keep(c).start()

    barrier = pltpu.get_barrier_semaphore()
    for dst in ((pp, peer), (other_pp, tp), (other_pp, peer)):
        pl.semaphore_signal(barrier, inc=1, device_id=dst, device_id_type=MESH)
    pl.semaphore_wait(barrier, 3)

    @pl.when(sends_b)
    def _():
        for c in range(2):
            for blk in range(2):
                x_send(c, blk, (other_pp, blk)).start()

    @pl.when(keeps_a)
    def _():
        for c in range(2):
            x_send(c, 0, (pp, 0)).start()

    zrow = jnp.zeros((row, ch), xs.dtype)
    zpos = jnp.zeros((nn, ch), xs.dtype)
    for b in range(3):
        xs[b, pl.ds(0, row), :] = zrow
        xs[b, pl.ds((hh + 1) * row, row), :] = zrow
    for h in range(hh):
        for b, wo in ((0, 0), (2, ww - 1)):
            xs[b, pl.ds((h + 1) * row + wo * nn, nn), :] = zpos
            xs[3 + b, pl.ds(h * row + wo * nn, nn), :] = zpos

    def stage(c):
        lo, hi = X_ROWS[c]

        @pl.when(keeps_a)
        def _():
            x_keep(c).wait()

        @pl.when(jnp.logical_not(keeps_a))
        def _():
            x_send(c, 0, (other_pp, 0)).wait_recv()

        def pair(hp, carry):
            base = pl.multiple_of(hp * (2 * row), 2 * row)
            for e in range(2):
                for wi in range(ww):
                    piece = xr[2 * hp + e, wi]
                    for b in range(3):
                        wo = wi + 1 - b
                        if 0 <= wo < ww:
                            off = e * row + wo * nn
                            xs.at[b, pl.ds(base, 3 * row), :][pl.ds(row + off, nn), :] = piece
                            xs.at[3 + b, pl.ds(base, 2 * row), :][pl.ds(off, nn), :] = piece
            return carry

        lax.fori_loop(lo // 2, hi // 2, pair, 0)

    def finish(s, j):
        lo, hi = OUT_ROWS[s]
        m = (hi - lo) * row
        p_send(s, j).wait_recv()
        pre = pown[j, pl.ds(0, m), :] + pr[s][j]
        y = pre * scale[j] + shift[j]
        zbuf[j, z_rows(s), :] = jnp.maximum(y, 0.0).astype(zbuf.dtype)

        @pl.when(on_s0)
        def _():
            z_send(s, j).start()

        @pl.when(on_s1)
        def _():
            z_keep(s, j).start()

    def step(s, j, has_next):
        lo, hi = OUT_ROWS[s]
        m = (hi - lo) * row
        turn = s * nj + j
        slot = lax.rem(turn, 2)
        for copy in w_copies(j, slot):
            copy.wait()

        @pl.when(has_next)
        def _():
            for copy in w_copies(lax.rem(j + 1, nj), 1 - slot):
                copy.start()

        acc = None
        for a in range(3):
            for b in range(3):
                if a == 1:
                    lhs = xs[3 + b, pl.ds(lo * row, m), :]
                else:
                    lhs = xs[b, pl.ds((lo + a) * row, m), :]
                term = jnp.dot(lhs, wbuf[slot, 3 * a + b], preferred_element_type=jnp.float32)
                acc = term if acc is None else acc + term
        ps[s][j] = acc[:, TILE:]
        pown[j, pl.ds(0, m), :] = acc[:, :TILE]
        p_send(s, j).start()

    def strip(s):
        def body(j, carry):
            step(s, j, s * nj + j + 1 < 2 * nj)

            @pl.when(j > 0)
            def _():
                finish(s, j - 1)

            return carry

        lax.fori_loop(0, nj, body, 0)

    stage(0)
    strip(0)
    stage(1)
    finish(0, nj - 1)
    strip(1)
    finish(1, nj - 1)

    for s in range(2):
        for j in range(nj):
            p_send(s, j).wait_send()

    @pl.when(sends_b)
    def _():
        for c in range(2):
            for blk in range(2):
                x_send(c, blk, (other_pp, blk)).wait_send()

    @pl.when(keeps_a)
    def _():
        for c in range(2):
            x_send(c, 0, (pp, 0)).wait_send()

    @pl.when(on_s0)
    def _():
        for s in range(2):
            for j in range(nj):
                z_send(s, j).wait_send()

    @pl.when(on_s1)
    def _():
        for s in range(2):
            for j in range(nj):
                z_keep(s, j).wait()
                z_send(s, j).wait_recv()


def weave_kernel(half, zb, za, out):
    on_s1 = lax.axis_index("pp") >= half
    nj, rows, tile = zb.shape
    nn = out.shape[1] // 2

    @pl.when(on_s1)
    def _():
        for j in range(nj):
            cols = pl.ds(j * tile, tile)
            for i in range(rows // nn):
                out[i, pl.ds(0, nn), cols] = zb[j, pl.ds(i * nn, nn), :]
                out[i, pl.ds(nn, nn), cols] = za[j, pl.ds(i * nn, nn), :]

    @pl.when(jnp.logical_not(on_s1))
    def _():
        out[...] = jnp.zeros_like(out)


def solution(mesh):
    half = mesh.shape["pp"] // 2

    def local_step(act, w, scale, shift):
        nn, hh, ww, cc = act.shape
        ch = cc // 2
        nj = ch // TILE
        row = ww * nn
        x = act.transpose(1, 2, 0, 3)
        w = w.reshape(9, ch, cc)
        m0, m1 = ((hi - lo) * row for lo, hi in OUT_ROWS)
        anyspec = pl.BlockSpec(memory_space=pl.ANY)
        vspec = pl.BlockSpec(memory_space=pltpu.VMEM)
        z_shape = jax.ShapeDtypeStruct((nj, hh * row, TILE), jnp.bfloat16)
        dma = pltpu.SemaphoreType.DMA
        zb, za = pl.pallas_call(
            functools.partial(conv_kernel, half),
            out_shape=(z_shape, z_shape),
            in_specs=[anyspec, anyspec, vspec, vspec],
            out_specs=(anyspec, anyspec),
            scratch_shapes=[
                pltpu.VMEM((hh, ww, nn, ch), jnp.bfloat16),
                pltpu.VMEM((6, (hh + 2) * row, ch), jnp.bfloat16),
                pltpu.VMEM((2, 9, ch, 2 * TILE), jnp.bfloat16),
                pltpu.VMEM((nj, m0, TILE), jnp.float32),
                pltpu.VMEM((nj, m1, TILE), jnp.float32),
                pltpu.VMEM((nj, m0, TILE), jnp.float32),
                pltpu.VMEM((nj, m1, TILE), jnp.float32),
                pltpu.VMEM((nj, max(m0, m1), TILE), jnp.float32),
                pltpu.VMEM((nj, hh * row, TILE), jnp.bfloat16),
                dma((2, 2)), dma((2,)), dma((2,)), dma((2, 2)),
                dma((2, nj)), dma((2, nj)), dma((2, nj)), dma((2, nj)), dma((2, nj)),
            ],
            compiler_params=pltpu.CompilerParams(collective_id=0, has_side_effects=True, vmem_limit_bytes=VMEM_LIMIT),
        )(x, w, scale.reshape(nj, 1, TILE), shift.reshape(nj, 1, TILE))
        blk = 2 * row
        out = pl.pallas_call(
            functools.partial(weave_kernel, half),
            grid=(hh * row // blk,),
            out_shape=jax.ShapeDtypeStruct((hh * ww, 2 * nn, ch), jnp.bfloat16),
            in_specs=[pl.BlockSpec((nj, blk, TILE), lambda i: (0, i, 0))] * 2,
            out_specs=pl.BlockSpec((blk // nn, 2 * nn, ch), lambda i: (i, 0, 0)),
        )(zb, za)
        return out.reshape(hh, ww, 2 * nn, ch).transpose(2, 0, 1, 3)

    return jax.shard_map(local_step, mesh=mesh, in_specs=(P(("pp", "tp")), P(None, None, "tp", None), P("tp"), P("tp")), out_specs=P("pp", None, None, "tp"), check_vma=False)
```

profile of v0, /device:TPU:64, one launch (start us, length us, event | category | flops | bytes accessed | tf_op | source)
XLA Modules:
  0.0 112.7 jit_solution(12538559000585544142)
XLA Ops:
  0.0 1.3 %reshape.13.scale = f32[5,1,256]{2,1,0:T(1,128)} reshape(f32[1280]{0:T(1024)} %param.6) | data formatting | bytes 10240 | tf_op jit(solution)/shard_map/reshape | solution.py:268
  1.3 1.3 %reshape.14.shift = f32[5,1,256]{2,1,0:T(1,128)} reshape(f32[1280]{0:T(1024)} %param.7) | data formatting | bytes 10240 | tf_op jit(solution)/shard_map/reshape | solution.py:268
  2.6 103.6 %shard_map.46 = (bf16[5,784,256]{2,1,0:T(8,128)(2,1)}, bf16[5,784,256]{2,1,0:T(8,128)(2,1)}) custom-call(bf16[14,14,4,2560]{3,2,1,0:T(4,128)(2,1)} %bitcast.6, bf16[9,1280,2560]{2,1,0:T(8,128)(2,1)} %bitcast.5, f32[5,1,256]{2,1,0:T(1,128)} %reshape.13.scale, f32[5,1,256]{2,1,0:T(1,128)} %reshape.14.shift), custom_call_target="tpu_custom_call" | custom-call | tf_op jit(solution)/shard_map/pallas_call | solution.py:249
  106.2 6.4 %shard_map.47 = bf16[196,8,1280]{2,1,0:T(8,128)(2,1)} custom-call(bf16[5,784,256]{2,1,0:T(8,128)(2,1)} %get-tuple-element.7.zb, bf16[5,784,256]{2,1,0:T(8,128)(2,1)} %get-tuple-element.8.za), custom_call_target="tpu_custom_call" | custom-call | tf_op jit(solution)/shard_map/pallas_call | solution.py:270
where the time goes:
time: 113 us
  Pallas kernels  110 us (97%)
  local copies, waits for them, and re-layouts  2.6 us (2%)
    pallas_call x1, Pallas kernels, local_step(): pl.pallas_call(functools.partial(conv_kernel, half), out_shape=(z_shape,...  104 us
    pallas_call x1, Pallas kernels, local_step(): pl.pallas_call(functools.partial(weave_kernel, half), grid=(hh * row // b...  6.45 us

commit v1 on v0

--- a/solution.py
+++ b/solution.py
@@ -11,11 +11,12 @@
 TILE = 256
 X_ROWS = ((0, 8), (8, 14))
 OUT_ROWS = ((0, 6), (6, 14))
-VMEM_LIMIT = 67043328
-
-
-def conv_kernel(half, x, w, scale, shift, zb, za, xr, xs, wbuf, ps0, ps1, pr0, pr1, pown, zbuf,
-                xsend, xrecv, xloc, wsem, psend, precv, zsend, zrecv, zloc):
+HOLD = 3
+VMEM_LIMIT = 62000000
+
+
+def conv_kernel(half, x, w, scale, shift, out, xr, xs, wbuf, ps0, ps1, pr0, pr1, pown, zbuf, za,
+                xsend, xrecv, xloc, wsem, psend, precv, zsend, zrecv):
     pp, tp = lax.axis_index("pp"), lax.axis_index("tp")
     on_s1 = pp >= half
     on_s0 = jnp.logical_not(on_s1)
@@ -27,6 +28,7 @@
     ch = cc // 2
     row = ww * nn
     nj = ch // TILE
+    hold = min(HOLD, nj - 1)
     ps, pr = (ps0, ps1), (pr0, pr1)
 
     def w_copies(j, slot):
@@ -60,8 +62,14 @@
             src_ref=zbuf.at[j, z_rows(s)], dst_ref=za.at[j, z_rows(s)], send_sem=zsend.at[s, j], recv_sem=zrecv.at[s, j],
             device_id=(other_pp, tp), device_id_type=MESH)
 
-    def z_keep(s, j):
-        return pltpu.make_async_copy(zbuf.at[j, z_rows(s)], zb.at[j, z_rows(s)], zloc.at[s, j])
+    def weave(s, j, src, group):
+        lo, hi = OUT_ROWS[s]
+        cols = pl.ds(pl.multiple_of(j * TILE, TILE), TILE)
+        for k in range(lo * ww, hi * ww):
+            out[k, pl.ds(group * nn, nn), cols] = src[j, pl.ds(k * nn, nn), :]
+
+    def channel(ref, j):
+        return jnp.concatenate([ref[pl.ds(2 * j, 1), :], ref[pl.ds(2 * j + 1, 1), :]], axis=1)
 
     for copy in w_copies(0, 0):
         copy.start()
@@ -86,6 +94,10 @@
     def _():
         for c in range(2):
             x_send(c, 0, (pp, 0)).start()
+
+    @pl.when(on_s0)
+    def _():
+        out[...] = jnp.zeros_like(out)
 
     zrow = jnp.zeros((row, ch), xs.dtype)
     zpos = jnp.zeros((nn, ch), xs.dtype)
@@ -123,21 +135,23 @@
 
         lax.fori_loop(lo // 2, hi // 2, pair, 0)
 
-    def finish(s, j):
+    def finish(s, j, held=None):
         lo, hi = OUT_ROWS[s]
         m = (hi - lo) * row
         p_send(s, j).wait_recv()
         pre = pown[j, pl.ds(0, m), :] + pr[s][j]
-        y = pre * scale[j] + shift[j]
+        y = pre * channel(scale, j) + channel(shift, j)
         zbuf[j, z_rows(s), :] = jnp.maximum(y, 0.0).astype(zbuf.dtype)
 
-        @pl.when(on_s0)
+        now = on_s0 if held is None else jnp.logical_and(on_s0, jnp.logical_or(tp == 0, jnp.logical_not(held)))
+
+        @pl.when(now)
         def _():
             z_send(s, j).start()
 
         @pl.when(on_s1)
         def _():
-            z_keep(s, j).start()
+            weave(s, j, zbuf, 0)
 
     def step(s, j, has_next):
         lo, hi = OUT_ROWS[s]
@@ -167,11 +181,17 @@
 
     def strip(s):
         def body(j, carry):
+            if s == 1:
+                @pl.when(jnp.logical_and(keeps_a, j == hold))
+                def _():
+                    for s2, j2 in [(0, i) for i in range(nj)] + [(1, i) for i in range(hold - 1)]:
+                        z_send(s2, j2).start()
+
             step(s, j, s * nj + j + 1 < 2 * nj)
 
             @pl.when(j > 0)
             def _():
-                finish(s, j - 1)
+                finish(s, j - 1, jnp.logical_or(s == 0, j - 1 < hold - 1))
 
             return carry
 
@@ -180,7 +200,7 @@
     stage(0)
     strip(0)
     stage(1)
-    finish(0, nj - 1)
+    finish(0, nj - 1, True)
     strip(1)
     finish(1, nj - 1)
 
@@ -209,26 +229,8 @@
     def _():
         for s in range(2):
             for j in range(nj):
-                z_keep(s, j).wait()
                 z_send(s, j).wait_recv()
-
-
-def weave_kernel(half, zb, za, out):
-    on_s1 = lax.axis_index("pp") >= half
-    nj, rows, tile = zb.shape
-    nn = out.shape[1] // 2
-
-    @pl.when(on_s1)
-    def _():
-        for j in range(nj):
-            cols = pl.ds(j * tile, tile)
-            for i in range(rows // nn):
-                out[i, pl.ds(0, nn), cols] = zb[j, pl.ds(i * nn, nn), :]
-                out[i, pl.ds(nn, nn), cols] = za[j, pl.ds(i * nn, nn), :]
-
-    @pl.when(jnp.logical_not(on_s1))
-    def _():
-        out[...] = jnp.zeros_like(out)
+                weave(s, j, za, 1)
 
 
 def solution(mesh):
@@ -244,13 +246,12 @@
         m0, m1 = ((hi - lo) * row for lo, hi in OUT_ROWS)
         anyspec = pl.BlockSpec(memory_space=pl.ANY)
         vspec = pl.BlockSpec(memory_space=pltpu.VMEM)
-        z_shape = jax.ShapeDtypeStruct((nj, hh * row, TILE), jnp.bfloat16)
         dma = pltpu.SemaphoreType.DMA
-        zb, za = pl.pallas_call(
+        out = pl.pallas_call(
             functools.partial(conv_kernel, half),
-            out_shape=(z_shape, z_shape),
+            out_shape=pltpu.VMEM((hh * ww, 2 * nn, ch), jnp.bfloat16),
             in_specs=[anyspec, anyspec, vspec, vspec],
-            out_specs=(anyspec, anyspec),
+            out_specs=vspec,
             scratch_shapes=[
                 pltpu.VMEM((hh, ww, nn, ch), jnp.bfloat16),
                 pltpu.VMEM((6, (hh + 2) * row, ch), jnp.bfloat16),
@@ -261,19 +262,12 @@
                 pltpu.VMEM((nj, m1, TILE), jnp.float32),
                 pltpu.VMEM((nj, max(m0, m1), TILE), jnp.float32),
                 pltpu.VMEM((nj, hh * row, TILE), jnp.bfloat16),
+                pltpu.VMEM((nj, hh * row, TILE), jnp.bfloat16),
                 dma((2, 2)), dma((2,)), dma((2,)), dma((2, 2)),
-                dma((2, nj)), dma((2, nj)), dma((2, nj)), dma((2, nj)), dma((2, nj)),
+                dma((2, nj)), dma((2, nj)), dma((2, nj)), dma((2, nj)),
             ],
             compiler_params=pltpu.CompilerParams(collective_id=0, has_side_effects=True, vmem_limit_bytes=VMEM_LIMIT),
-        )(x, w, scale.reshape(nj, 1, TILE), shift.reshape(nj, 1, TILE))
-        blk = 2 * row
-        out = pl.pallas_call(
-            functools.partial(weave_kernel, half),
-            grid=(hh * row // blk,),
-            out_shape=jax.ShapeDtypeStruct((hh * ww, 2 * nn, ch), jnp.bfloat16),
-            in_specs=[pl.BlockSpec((nj, blk, TILE), lambda i: (0, i, 0))] * 2,
-            out_specs=pl.BlockSpec((blk // nn, 2 * nn, ch), lambda i: (i, 0, 0)),
-        )(zb, za)
+        )(x, w, scale.reshape(2 * nj, TILE // 2), shift.reshape(2 * nj, TILE // 2))
         return out.reshape(hh, ww, 2 * nn, ch).transpose(2, 0, 1, 3)
 
     return jax.shard_map(local_step, mesh=mesh, in_specs=(P(("pp", "tp")), P(None, None, "tp", None), P("tp"), P("tp")), out_specs=P("pp", None, None, "tp"), check_vma=False)

time: 113 us -> 95.6 us (0.85)
  the two profiles are of different devices: /device:TPU:64 before, /device:TPU:1 now
where the time goes in v1:
time: 95.6 us; the launch traced here: 95.4 us
  Pallas kernels  93.5 us (98%)
  local copies, waits for them, and re-layouts  1.95 us (2%)
    pallas_call x1, Pallas kernels, local_step(): pl.pallas_call(functools.partial(conv_kernel, half), out_shape=pltpu.VMEM...  93.5 us
    unnamed x1, local copies, waits for them, and re-layouts  1.95 us

profile of v1, /device:TPU:1, one launch (start us, length us, event | category | flops | bytes accessed | tf_op | source)
XLA Modules:
  0.0 95.4 jit_solution(281780832199370717)
XLA Ops:
  0.0 93.5 %shard_map.46 = bf16[196,8,1280]{2,1,0:T(8,128)(2,1)S(1)} custom-call(bf16[14,14,4,2560]{3,2,1,0:T(4,128)(2,1)} %bitcast.9, bf16[9,1280,2560]{2,1,0:T(8,128)(2,1)} %bitcast.8, f32[10,128]{1,0:T(8,128)} %bitcast.10, f32[10,128]{1,0:T(8,128)} %bitcast.11), custom_call_target="tpu_custom_call" | custom-call | tf_op jit(solution)/shard_map/pallas_call | solution.py:250
  93.5 2.0 %copy.6 = bf16[8,14,14,1280]{3,0,2,1:T(8,128)(2,1)} copy(bf16[8,14,14,1280]{3,0,2,1:T(8,128)(2,1)S(1)} %bitcast.7) | data formatting | bytes 8028160

commit v2 on v1

--- a/solution.py
+++ b/solution.py
@@ -9,14 +9,15 @@
 
 MESH = pl.DeviceIdType.MESH
 TILE = 256
-X_ROWS = ((0, 8), (8, 14))
+X_ROWS = ((0, 2), (2, 8), (8, 14))
+STAGED = ((0, 1), (2,))
 OUT_ROWS = ((0, 6), (6, 14))
-HOLD = 3
+HOLD = 2
 VMEM_LIMIT = 62000000
 
 
-def conv_kernel(half, x, w, scale, shift, out, xr, xs, wbuf, ps0, ps1, pr0, pr1, pown, zbuf, za,
-                xsend, xrecv, xloc, wsem, psend, precv, zsend, zrecv):
+def conv_kernel(half, x, w, scale_in, shift_in, out, scale, shift, first, xr, xs, wbuf, ps0, ps1, pr0, pr1, pown, zbuf, za,
+                csem, fsem, xsend, xrecv, xloc, wsem, psend, precv, zsend, zrecv):
     pp, tp = lax.axis_index("pp"), lax.axis_index("tp")
     on_s1 = pp >= half
     on_s0 = jnp.logical_not(on_s1)
@@ -36,10 +37,10 @@
             cols = pl.ds(pl.multiple_of(blk * ch + j * TILE, TILE), TILE)
             yield pltpu.make_async_copy(w.at[:, :, cols], wbuf.at[slot, :, :, pl.ds(k * TILE, TILE)], wsem.at[slot, k])
 
-    def x_send(c, blk, dst):
+    def x_send(c, blk, dst, from_vmem=False):
         lo, hi = X_ROWS[c]
         return pltpu.make_async_remote_copy(
-            src_ref=x.at[pl.ds(lo, hi - lo), :, :, pl.ds(blk * ch, ch)],
+            src_ref=first if from_vmem else x.at[pl.ds(lo, hi - lo), :, :, pl.ds(blk * ch, ch)],
             dst_ref=xr.at[pl.ds(lo, hi - lo)],
             send_sem=xsend.at[c, blk], recv_sem=xrecv.at[c],
             device_id=dst, device_id_type=MESH)
@@ -71,29 +72,44 @@
     def channel(ref, j):
         return jnp.concatenate([ref[pl.ds(2 * j, 1), :], ref[pl.ds(2 * j + 1, 1), :]], axis=1)
 
-    for copy in w_copies(0, 0):
-        copy.start()
-
-    @pl.when(keeps_a)
-    def _():
-        for c in range(2):
-            x_keep(c).start()
-
     barrier = pltpu.get_barrier_semaphore()
     for dst in ((pp, peer), (other_pp, tp), (other_pp, peer)):
         pl.semaphore_signal(barrier, inc=1, device_id=dst, device_id_type=MESH)
+
+    load_first = pltpu.make_async_copy(x.at[pl.ds(0, X_ROWS[0][1]), :, :, pl.ds(0, ch)], first, fsem)
+
+    @pl.when(sends_b)
+    def _():
+        load_first.start()
+
+    @pl.when(keeps_a)
+    def _():
+        for c in range(len(X_ROWS)):
+            x_keep(c).start()
+
+    channel_copies = [pltpu.make_async_copy(scale_in, scale, csem.at[0]), pltpu.make_async_copy(shift_in, shift, csem.at[1])]
+    for copy in [*w_copies(0, 0), *channel_copies]:
+        copy.start()
+
+    @pl.when(sends_b)
+    def _():
+        load_first.wait()
+
     pl.semaphore_wait(barrier, 3)
-
-    @pl.when(sends_b)
-    def _():
-        for c in range(2):
-            for blk in range(2):
-                x_send(c, blk, (other_pp, blk)).start()
+    b_sends = [(c, blk) for cs in STAGED for blk in range(2) for c in cs]
+
+    @pl.when(sends_b)
+    def _():
+        for c, blk in b_sends:
+            x_send(c, blk, (other_pp, blk), (c, blk) == (0, 0)).start()
 
     @pl.when(keeps_a)
     def _():
-        for c in range(2):
+        for c in range(len(X_ROWS)):
             x_send(c, 0, (pp, 0)).start()
+
+    for copy in channel_copies:
+        copy.wait()
 
     @pl.when(on_s0)
     def _():
@@ -109,16 +125,18 @@
             xs[b, pl.ds((h + 1) * row + wo * nn, nn), :] = zpos
             xs[3 + b, pl.ds(h * row + wo * nn, nn), :] = zpos
 
-    def stage(c):
-        lo, hi = X_ROWS[c]
+    def stage(s):
+        lo, hi = X_ROWS[STAGED[s][0]][0], X_ROWS[STAGED[s][-1]][1]
 
         @pl.when(keeps_a)
         def _():
-            x_keep(c).wait()
+            for c in STAGED[s]:
+                x_keep(c).wait()
 
         @pl.when(jnp.logical_not(keeps_a))
         def _():
-            x_send(c, 0, (other_pp, 0)).wait_recv()
+            for c in STAGED[s]:
+                x_send(c, 0, (other_pp, 0)).wait_recv()
 
         def pair(hp, carry):
             base = pl.multiple_of(hp * (2 * row), 2 * row)
@@ -210,13 +228,12 @@
 
     @pl.when(sends_b)
     def _():
-        for c in range(2):
-            for blk in range(2):
-                x_send(c, blk, (other_pp, blk)).wait_send()
+        for c, blk in b_sends:
+            x_send(c, blk, (other_pp, blk), (c, blk) == (0, 0)).wait_send()
 
     @pl.when(keeps_a)
     def _():
-        for c in range(2):
+        for c in range(len(X_ROWS)):
             x_send(c, 0, (pp, 0)).wait_send()
 
     @pl.when(on_s0)
@@ -247,12 +264,16 @@
         anyspec = pl.BlockSpec(memory_space=pl.ANY)
         vspec = pl.BlockSpec(memory_space=pltpu.VMEM)
         dma = pltpu.SemaphoreType.DMA
+        npc = len(X_ROWS)
         out = pl.pallas_call(
             functools.partial(conv_kernel, half),
             out_shape=pltpu.VMEM((hh * ww, 2 * nn, ch), jnp.bfloat16),
-            in_specs=[anyspec, anyspec, vspec, vspec],
+            in_specs=[anyspec] * 4,
             out_specs=vspec,
             scratch_shapes=[
+                pltpu.VMEM((2 * nj, TILE // 2), jnp.float32),
+                pltpu.VMEM((2 * nj, TILE // 2), jnp.float32),
+                pltpu.VMEM((X_ROWS[0][1], ww, nn, ch), jnp.bfloat16),
                 pltpu.VMEM((hh, ww, nn, ch), jnp.bfloat16),
                 pltpu.VMEM((6, (hh + 2) * row, ch), jnp.bfloat16),
                 pltpu.VMEM((2, 9, ch, 2 * TILE), jnp.bfloat16),
@@ -263,7 +284,7 @@
                 pltpu.VMEM((nj, max(m0, m1), TILE), jnp.float32),
                 pltpu.VMEM((nj, hh * row, TILE), jnp.bfloat16),
                 pltpu.VMEM((nj, hh * row, TILE), jnp.bfloat16),
-                dma((2, 2)), dma((2,)), dma((2,)), dma((2, 2)),
+                dma((2,)), dma, dma((npc, 2)), dma((npc,)), dma((npc,)), dma((2, 2)),
                 dma((2, nj)), dma((2, nj)), dma((2, nj)), dma((2, nj)),
             ],
             compiler_params=pltpu.CompilerParams(collective_id=0, has_side_effects=True, vmem_limit_bytes=VMEM_LIMIT),

time: 95.6 us -> 94 us (0.983)
  the two profiles are of different devices: /device:TPU:1 before, /device:TPU:64 now
where the time goes in v2:
time: 94 us; the launch traced here: 93.9 us
  Pallas kernels  91.9 us (98%)
  local copies, waits for them, and re-layouts  1.95 us (2%)
    pallas_call x1, Pallas kernels, local_step(): pl.pallas_call(functools.partial(conv_kernel, half), out_shape=pltpu.VMEM...  91.9 us
    unnamed x1, local copies, waits for them, and re-layouts  1.95 us

profile of v2, /device:TPU:64, one launch (start us, length us, event | category | flops | bytes accessed | tf_op | source)
XLA Modules:
  0.0 93.9 jit_solution(6370739108327094267)
XLA Ops:
  0.0 91.9 %shard_map.46 = bf16[196,8,1280]{2,1,0:T(8,128)(2,1)S(1)} custom-call(bf16[14,14,4,2560]{3,2,1,0:T(4,128)(2,1)} %bitcast.9, bf16[9,1280,2560]{2,1,0:T(8,128)(2,1)} %bitcast.8, f32[10,128]{1,0:T(8,128)} %bitcast.10, f32[10,128]{1,0:T(8,128)} %bitcast.11), custom_call_target="tpu_custom_call" | custom-call | tf_op jit(solution)/shard_map/pallas_call | solution.py:268
  91.9 2.0 %copy.6 = bf16[8,14,14,1280]{3,0,2,1:T(8,128)(2,1)} copy(bf16[8,14,14,1280]{3,0,2,1:T(8,128)(2,1)S(1)} %bitcast.7) | data formatting | bytes 8028160

commit v3 on v2

--- a/solution.py
+++ b/solution.py
@@ -12,19 +12,20 @@
 X_ROWS = ((0, 2), (2, 8), (8, 14))
 STAGED = ((0, 1), (2,))
 OUT_ROWS = ((0, 6), (6, 14))
-HOLD = 2
+HOLD = 3
 VMEM_LIMIT = 62000000
 
 
 def conv_kernel(half, x, w, scale_in, shift_in, out, scale, shift, first, xr, xs, wbuf, ps0, ps1, pr0, pr1, pown, zbuf, za,
-                csem, fsem, xsend, xrecv, xloc, wsem, psend, precv, zsend, zrecv):
+                csem, fsem, late, xsend, xrecv, xloc, wsem, psend, precv, zsend, zrecv):
     pp, tp = lax.axis_index("pp"), lax.axis_index("tp")
     on_s1 = pp >= half
     on_s0 = jnp.logical_not(on_s1)
     other_pp = jnp.where(on_s1, pp - half, pp + half)
     peer = 1 - tp
-    sends_b = jnp.logical_and(on_s0, tp == 0)
-    keeps_a = jnp.logical_and(on_s0, tp == 1)
+    sends_b = jnp.logical_and(on_s0, tp == 1)
+    keeps_a = jnp.logical_and(on_s0, tp == 0)
+    late_core = jnp.logical_and(on_s1, tp == 0)
     hh, ww, nn, cc = x.shape
     ch = cc // 2
     row = ww * nn
@@ -47,7 +48,7 @@
 
     def x_keep(c):
         lo, hi = X_ROWS[c]
-        return pltpu.make_async_copy(x.at[pl.ds(lo, hi - lo), :, :, pl.ds(ch, ch)], xr.at[pl.ds(lo, hi - lo)], xloc.at[c])
+        return pltpu.make_async_copy(x.at[pl.ds(lo, hi - lo), :, :, pl.ds(0, ch)], xr.at[pl.ds(lo, hi - lo)], xloc.at[c])
 
     def p_send(s, j):
         return pltpu.make_async_remote_copy(
@@ -73,10 +74,17 @@
         return jnp.concatenate([ref[pl.ds(2 * j, 1), :], ref[pl.ds(2 * j + 1, 1), :]], axis=1)
 
     barrier = pltpu.get_barrier_semaphore()
-    for dst in ((pp, peer), (other_pp, tp), (other_pp, peer)):
-        pl.semaphore_signal(barrier, inc=1, device_id=dst, device_id_type=MESH)
-
-    load_first = pltpu.make_async_copy(x.at[pl.ds(0, X_ROWS[0][1]), :, :, pl.ds(0, ch)], first, fsem)
+    pl.semaphore_signal(barrier, inc=1, device_id=(pp, peer), device_id_type=MESH)
+
+    @pl.when(on_s1)
+    def _():
+        pl.semaphore_signal(barrier, inc=1, device_id=(other_pp, tp), device_id_type=MESH)
+
+    @pl.when(sends_b)
+    def _():
+        pl.semaphore_signal(barrier, inc=1, device_id=(other_pp, 0), device_id_type=MESH)
+
+    load_first = pltpu.make_async_copy(x.at[pl.ds(0, X_ROWS[0][1]), :, :, pl.ds(ch, ch)], first, fsem)
 
     @pl.when(sends_b)
     def _():
@@ -95,18 +103,25 @@
     def _():
         load_first.wait()
 
-    pl.semaphore_wait(barrier, 3)
-    b_sends = [(c, blk) for cs in STAGED for blk in range(2) for c in cs]
+    pl.semaphore_wait(barrier, jnp.where(jnp.logical_and(on_s1, tp == 1), 1, 2))
+
+    @pl.when(late_core)
+    def _():
+        pl.semaphore_signal(late, inc=1, device_id=(other_pp, 1), device_id_type=MESH)
+
+    b_sends = [(c, blk) for cs in STAGED for blk in (1, 0) for c in cs]
 
     @pl.when(sends_b)
     def _():
         for c, blk in b_sends:
-            x_send(c, blk, (other_pp, blk), (c, blk) == (0, 0)).start()
+            if (c, blk) == (0, 0):
+                pl.semaphore_wait(late, 1)
+            x_send(c, blk, (other_pp, blk), (c, blk) == (0, 1)).start()
 
     @pl.when(keeps_a)
     def _():
         for c in range(len(X_ROWS)):
-            x_send(c, 0, (pp, 0)).start()
+            x_send(c, 1, (pp, 1)).start()
 
     for copy in channel_copies:
         copy.wait()
@@ -161,7 +176,7 @@
         y = pre * channel(scale, j) + channel(shift, j)
         zbuf[j, z_rows(s), :] = jnp.maximum(y, 0.0).astype(zbuf.dtype)
 
-        now = on_s0 if held is None else jnp.logical_and(on_s0, jnp.logical_or(tp == 0, jnp.logical_not(held)))
+        now = on_s0 if held is None else jnp.logical_and(on_s0, jnp.logical_or(tp == 1, jnp.logical_not(held)))
 
         @pl.when(now)
         def _():
@@ -169,7 +184,7 @@
 
         @pl.when(on_s1)
         def _():
-            weave(s, j, zbuf, 0)
+            weave(s, j, zbuf, 1)
 
     def step(s, j, has_next):
         lo, hi = OUT_ROWS[s]
@@ -229,12 +244,12 @@
     @pl.when(sends_b)
     def _():
         for c, blk in b_sends:
-            x_send(c, blk, (other_pp, blk), (c, blk) == (0, 0)).wait_send()
+            x_send(c, blk, (other_pp, blk), (c, blk) == (0, 1)).wait_send()
 
     @pl.when(keeps_a)
     def _():
         for c in range(len(X_ROWS)):
-            x_send(c, 0, (pp, 0)).wait_send()
+            x_send(c, 1, (pp, 1)).wait_send()
 
     @pl.when(on_s0)
     def _():
@@ -247,7 +262,7 @@
         for s in range(2):
             for j in range(nj):
                 z_send(s, j).wait_recv()
-                weave(s, j, za, 1)
+                weave(s, j, za, 0)
 
 
 def solution(mesh):
@@ -284,7 +299,7 @@
                 pltpu.VMEM((nj, max(m0, m1), TILE), jnp.float32),
                 pltpu.VMEM((nj, hh * row, TILE), jnp.bfloat16),
                 pltpu.VMEM((nj, hh * row, TILE), jnp.bfloat16),
-                dma((2,)), dma, dma((npc, 2)), dma((npc,)), dma((npc,)), dma((2, 2)),
+                dma((2,)), dma, pltpu.SemaphoreType.REGULAR, dma((npc, 2)), dma((npc,)), dma((npc,)), dma((2, 2)),
                 dma((2, nj)), dma((2, nj)), dma((2, nj)), dma((2, nj)),
             ],
             compiler_params=pltpu.CompilerParams(collective_id=0, has_side_effects=True, vmem_limit_bytes=VMEM_LIMIT),

time: 94 us -> 92.8 us (0.987)
  Pallas kernels: 91.9 us -> 90.8 us
    pallas_call x1, Pallas kernels: 91.9 us -> 90.8 us  [local_step(): pl.pallas_call(functools.partial(conv_kernel, half), out_shape=pltpu.VMEM...]
where the time goes in v3:
time: 92.8 us; the launch traced here: 92.7 us
  Pallas kernels  90.8 us (98%)
  local copies, waits for them, and re-layouts  1.95 us (2%)
    pallas_call x1, Pallas kernels, local_step(): pl.pallas_call(functools.partial(conv_kernel, half), out_shape=pltpu.VMEM...  90.8 us
    unnamed x1, local copies, waits for them, and re-layouts  1.95 us

profile of v3, /device:TPU:64, one launch (start us, length us, event | category | flops | bytes accessed | tf_op | source)
XLA Modules:
  0.0 92.7 jit_solution(18395610059471284612)
XLA Ops:
  0.0 90.8 %shard_map.46 = bf16[196,8,1280]{2,1,0:T(8,128)(2,1)S(1)} custom-call(bf16[14,14,4,2560]{3,2,1,0:T(4,128)(2,1)} %bitcast.9, bf16[9,1280,2560]{2,1,0:T(8,128)(2,1)} %bitcast.8, f32[10,128]{1,0:T(8,128)} %bitcast.10, f32[10,128]{1,0:T(8,128)} %bitcast.11), custom_call_target="tpu_custom_call" | custom-call | tf_op jit(solution)/shard_map/pallas_call | solution.py:283
  90.8 2.0 %copy.6 = bf16[8,14,14,1280]{3,0,2,1:T(8,128)(2,1)} copy(bf16[8,14,14,1280]{3,0,2,1:T(8,128)(2,1)S(1)} %bitcast.7) | data formatting | bytes 8028160

commit v4 on v3

--- a/solution.py
+++ b/solution.py
@@ -30,7 +30,7 @@
     ch = cc // 2
     row = ww * nn
     nj = ch // TILE
-    hold = min(HOLD, nj - 1)
+    hold = HOLD
     ps, pr = (ps0, ps1), (pr0, pr1)
 
     def w_copies(j, slot):
@@ -74,11 +74,12 @@
         return jnp.concatenate([ref[pl.ds(2 * j, 1), :], ref[pl.ds(2 * j + 1, 1), :]], axis=1)
 
     barrier = pltpu.get_barrier_semaphore()
+
+    @pl.when(on_s1)
+    def _():
+        pl.semaphore_signal(barrier, inc=1, device_id=(other_pp, tp), device_id_type=MESH)
+
     pl.semaphore_signal(barrier, inc=1, device_id=(pp, peer), device_id_type=MESH)
-
-    @pl.when(on_s1)
-    def _():
-        pl.semaphore_signal(barrier, inc=1, device_id=(other_pp, tp), device_id_type=MESH)
 
     @pl.when(sends_b)
     def _():
@@ -168,19 +169,13 @@
 
         lax.fori_loop(lo // 2, hi // 2, pair, 0)
 
-    def finish(s, j, held=None):
+    def finish(s, j):
         lo, hi = OUT_ROWS[s]
         m = (hi - lo) * row
         p_send(s, j).wait_recv()
         pre = pown[j, pl.ds(0, m), :] + pr[s][j]
         y = pre * channel(scale, j) + channel(shift, j)
         zbuf[j, z_rows(s), :] = jnp.maximum(y, 0.0).astype(zbuf.dtype)
-
-        now = on_s0 if held is None else jnp.logical_and(on_s0, jnp.logical_or(tp == 1, jnp.logical_not(held)))
-
-        @pl.when(now)
-        def _():
-            z_send(s, j).start()
 
         @pl.when(on_s1)
         def _():
@@ -210,22 +205,32 @@
                 acc = term if acc is None else acc + term
         ps[s][j] = acc[:, TILE:]
         pown[j, pl.ds(0, m), :] = acc[:, :TILE]
-        p_send(s, j).start()
+
+    def start_z(s, j, when):
+        @pl.when(when)
+        def _():
+            z_send(s, j).start()
 
     def strip(s):
         def body(j, carry):
             if s == 1:
                 @pl.when(jnp.logical_and(keeps_a, j == hold))
                 def _():
-                    for s2, j2 in [(0, i) for i in range(nj)] + [(1, i) for i in range(hold - 1)]:
+                    for s2, j2 in [(0, i) for i in range(nj)] + [(1, i) for i in range(hold - 2)]:
                         z_send(s2, j2).start()
 
             step(s, j, s * nj + j + 1 < 2 * nj)
+
+            free = sends_b if s == 0 else jnp.logical_or(sends_b, jnp.logical_and(keeps_a, j >= hold))
+            start_z(s, j - 2, jnp.logical_and(free, j > 1))
+            if s == 1:
+                start_z(0, nj - 1, jnp.logical_and(sends_b, j == 0))
 
             @pl.when(j > 0)
             def _():
-                finish(s, j - 1, jnp.logical_or(s == 0, j - 1 < hold - 1))
-
+                finish(s, j - 1)
+
+            p_send(s, j).start()
             return carry
 
         lax.fori_loop(0, nj, body, 0)
@@ -233,8 +238,10 @@
     stage(0)
     strip(0)
     stage(1)
-    finish(0, nj - 1, True)
+    start_z(0, nj - 2, sends_b)
+    finish(0, nj - 1)
     strip(1)
+    start_z(1, nj - 2, on_s0)
     finish(1, nj - 1)
 
     for s in range(2):
@@ -253,6 +260,7 @@
 
     @pl.when(on_s0)
     def _():
+        z_send(1, nj - 1).start()
         for s in range(2):
             for j in range(nj):
                 z_send(s, j).wait_send()

time: 92.8 us -> 92.8 us (level)
  no operation moved by 1% of the time
where the time goes in v4:
time: 92.8 us; the launch traced here: 92.7 us
  Pallas kernels  90.8 us (98%)
  local copies, waits for them, and re-layouts  1.95 us (2%)
    pallas_call x1, Pallas kernels, local_step(): pl.pallas_call(functools.partial(conv_kernel, half), out_shape=pltpu.VMEM...  90.8 us
    unnamed x1, local copies, waits for them, and re-layouts  1.95 us

profile of v4, /device:TPU:64, one launch (start us, length us, event | category | flops | bytes accessed | tf_op | source)
XLA Modules:
  0.0 92.7 jit_solution(4693485254160654321)
XLA Ops:
  0.0 90.8 %shard_map.46 = bf16[196,8,1280]{2,1,0:T(8,128)(2,1)S(1)} custom-call(bf16[14,14,4,2560]{3,2,1,0:T(4,128)(2,1)} %bitcast.9, bf16[9,1280,2560]{2,1,0:T(8,128)(2,1)} %bitcast.8, f32[10,128]{1,0:T(8,128)} %bitcast.10, f32[10,128]{1,0:T(8,128)} %bitcast.11), custom_call_target="tpu_custom_call" | custom-call | tf_op jit(solution)/shard_map/pallas_call | solution.py:291
  90.8 2.0 %copy.6 = bf16[8,14,14,1280]{3,0,2,1:T(8,128)(2,1)} copy(bf16[8,14,14,1280]{3,0,2,1:T(8,128)(2,1)S(1)} %bitcast.7) | data formatting | bytes 8028160

commit v5 on v4

--- a/solution.py
+++ b/solution.py
@@ -36,36 +36,53 @@
     def w_copies(j, slot):
         for k, blk in enumerate((tp, peer)):
             cols = pl.ds(pl.multiple_of(blk * ch + j * TILE, TILE), TILE)
-            yield pltpu.make_async_copy(w.at[:, :, cols], wbuf.at[slot, :, :, pl.ds(k * TILE, TILE)], wsem.at[slot, k])
+            yield pltpu.make_async_copy(w.at[:, :, cols], wbuf.at[slot, :, :, pl.ds(k * TILE, TILE)], wsem.at[slot])
+
+    def x_copy(lo, hi, s, blk, dst, src=None):
+        return pltpu.make_async_remote_copy(
+            src_ref=x.at[pl.ds(lo, hi - lo), :, :, pl.ds(blk * ch, ch)] if src is None else src,
+            dst_ref=xr.at[pl.ds(lo, hi - lo)],
+            send_sem=xsend.at[blk], recv_sem=xrecv.at[s],
+            device_id=dst, device_id_type=MESH)
 
     def x_send(c, blk, dst, from_vmem=False):
-        lo, hi = X_ROWS[c]
-        return pltpu.make_async_remote_copy(
-            src_ref=first if from_vmem else x.at[pl.ds(lo, hi - lo), :, :, pl.ds(blk * ch, ch)],
-            dst_ref=xr.at[pl.ds(lo, hi - lo)],
-            send_sem=xsend.at[c, blk], recv_sem=xrecv.at[c],
-            device_id=dst, device_id_type=MESH)
-
-    def x_keep(c):
-        lo, hi = X_ROWS[c]
-        return pltpu.make_async_copy(x.at[pl.ds(lo, hi - lo), :, :, pl.ds(0, ch)], xr.at[pl.ds(lo, hi - lo)], xloc.at[c])
+        s = 0 if c in STAGED[0] else 1
+        return x_copy(*X_ROWS[c], s, blk, dst, first if from_vmem else None)
+
+    def staged_rows(s):
+        return X_ROWS[STAGED[s][0]][0], X_ROWS[STAGED[s][-1]][1]
+
+    def x_keep(s):
+        lo, hi = staged_rows(s)
+        return pltpu.make_async_copy(x.at[pl.ds(lo, hi - lo), :, :, pl.ds(0, ch)], xr.at[pl.ds(lo, hi - lo)], xloc.at[s])
 
     def p_send(s, j):
         return pltpu.make_async_remote_copy(
-            src_ref=ps[s].at[j], dst_ref=pr[s].at[j], send_sem=psend.at[s, j], recv_sem=precv.at[s, j],
+            src_ref=ps[s].at[j], dst_ref=pr[s].at[j], send_sem=psend.at[s], recv_sem=precv.at[s, j],
             device_id=(pp, peer), device_id_type=MESH)
 
     def z_rows(s):
         lo, hi = OUT_ROWS[s]
         return pl.ds(lo * row, (hi - lo) * row)
 
+    def z_copy(tiles, rows, group):
+        return pltpu.make_async_remote_copy(
+            src_ref=zbuf.at[tiles, rows], dst_ref=za.at[tiles, rows], send_sem=zsend, recv_sem=zrecv.at[group],
+            device_id=(other_pp, tp), device_id_type=MESH)
+
     def z_send(s, j):
-        return pltpu.make_async_remote_copy(
-            src_ref=zbuf.at[j, z_rows(s)], dst_ref=za.at[j, z_rows(s)], send_sem=zsend.at[s, j], recv_sem=zrecv.at[s, j],
-            device_id=(other_pp, tp), device_id_type=MESH)
-
-    def weave(s, j, src, group):
-        lo, hi = OUT_ROWS[s]
+        return z_copy(j, z_rows(s), s)
+
+    last_lo, last_hi = OUT_ROWS[1]
+    last_mid = (last_lo + last_hi) // 2
+    halves = ((last_lo, last_mid), (last_mid, last_hi))
+
+    def z_last(i):
+        lo, hi = halves[i]
+        return z_copy(nj - 1, pl.ds(lo * row, (hi - lo) * row), 2 + i)
+
+    def weave(rows, j, src, group):
+        lo, hi = rows
         cols = pl.ds(pl.multiple_of(j * TILE, TILE), TILE)
         for k in range(lo * ww, hi * ww):
             out[k, pl.ds(group * nn, nn), cols] = src[j, pl.ds(k * nn, nn), :]
@@ -93,8 +110,8 @@
 
     @pl.when(keeps_a)
     def _():
-        for c in range(len(X_ROWS)):
-            x_keep(c).start()
+        for s in range(2):
+            x_keep(s).start()
 
     channel_copies = [pltpu.make_async_copy(scale_in, scale, csem.at[0]), pltpu.make_async_copy(shift_in, shift, csem.at[1])]
     for copy in [*w_copies(0, 0), *channel_copies]:
@@ -142,17 +159,15 @@
             xs[3 + b, pl.ds(h * row + wo * nn, nn), :] = zpos
 
     def stage(s):
-        lo, hi = X_ROWS[STAGED[s][0]][0], X_ROWS[STAGED[s][-1]][1]
+        lo, hi = staged_rows(s)
 
         @pl.when(keeps_a)
         def _():
-            for c in STAGED[s]:
-                x_keep(c).wait()
+            x_keep(s).wait()
 
         @pl.when(jnp.logical_not(keeps_a))
         def _():
-            for c in STAGED[s]:
-                x_send(c, 0, (other_pp, 0)).wait_recv()
+            x_copy(lo, hi, s, 0, (other_pp, 0)).wait_recv()
 
         def pair(hp, carry):
             base = pl.multiple_of(hp * (2 * row), 2 * row)
@@ -179,15 +194,14 @@
 
         @pl.when(on_s1)
         def _():
-            weave(s, j, zbuf, 1)
+            weave(OUT_ROWS[s], j, zbuf, 1)
 
     def step(s, j, has_next):
         lo, hi = OUT_ROWS[s]
         m = (hi - lo) * row
         turn = s * nj + j
         slot = lax.rem(turn, 2)
-        for copy in w_copies(j, slot):
-            copy.wait()
+        pltpu.make_async_copy(w.at[:, :, pl.ds(0, 2 * TILE)], wbuf.at[slot], wsem.at[slot]).wait()
 
         @pl.when(has_next)
         def _():
@@ -245,32 +259,34 @@
     finish(1, nj - 1)
 
     for s in range(2):
-        for j in range(nj):
-            p_send(s, j).wait_send()
-
-    @pl.when(sends_b)
-    def _():
-        for c, blk in b_sends:
-            x_send(c, blk, (other_pp, blk), (c, blk) == (0, 1)).wait_send()
+        pltpu.make_async_remote_copy(
+            src_ref=ps[s], dst_ref=pr[s], send_sem=psend.at[s], recv_sem=precv.at[s, 0],
+            device_id=(pp, peer), device_id_type=MESH).wait_send()
+
+    @pl.when(sends_b)
+    def _():
+        for blk in range(2):
+            x_copy(0, hh, 0, blk, (other_pp, blk)).wait_send()
 
     @pl.when(keeps_a)
     def _():
-        for c in range(len(X_ROWS)):
-            x_send(c, 1, (pp, 1)).wait_send()
+        x_copy(0, hh, 0, 1, (pp, 1)).wait_send()
 
     @pl.when(on_s0)
     def _():
-        z_send(1, nj - 1).start()
-        for s in range(2):
-            for j in range(nj):
-                z_send(s, j).wait_send()
+        for i in range(2):
+            z_last(i).start()
+        z_copy(pl.ds(0, nj), pl.ds(0, hh * row), 0).wait_send()
 
     @pl.when(on_s1)
     def _():
-        for s in range(2):
-            for j in range(nj):
-                z_send(s, j).wait_recv()
-                weave(s, j, za, 0)
+        for s, n in ((0, nj), (1, nj - 1)):
+            z_copy(pl.ds(0, n), z_rows(s), s).wait_recv()
+            for j in range(n):
+                weave(OUT_ROWS[s], j, za, 0)
+        for i in range(2):
+            z_last(i).wait_recv()
+            weave(halves[i], nj - 1, za, 0)
 
 
 def solution(mesh):
@@ -287,7 +303,6 @@
         anyspec = pl.BlockSpec(memory_space=pl.ANY)
         vspec = pl.BlockSpec(memory_space=pltpu.VMEM)
         dma = pltpu.SemaphoreType.DMA
-        npc = len(X_ROWS)
         out = pl.pallas_call(
             functools.partial(conv_kernel, half),
             out_shape=pltpu.VMEM((hh * ww, 2 * nn, ch), jnp.bfloat16),
@@ -307,8 +322,8 @@
                 pltpu.VMEM((nj, max(m0, m1), TILE), jnp.float32),
                 pltpu.VMEM((nj, hh * row, TILE), jnp.bfloat16),
                 pltpu.VMEM((nj, hh * row, TILE), jnp.bfloat16),
-                dma((2,)), dma, pltpu.SemaphoreType.REGULAR, dma((npc, 2)), dma((npc,)), dma((npc,)), dma((2, 2)),
-                dma((2, nj)), dma((2, nj)), dma((2, nj)), dma((2, nj)),
+                dma((2,)), dma, pltpu.SemaphoreType.REGULAR, dma((2,)), dma((2,)), dma((2,)), dma((2,)),
+                dma((2,)), dma((2, nj)), dma, dma((4,)),
             ],
             compiler_params=pltpu.CompilerParams(collective_id=0, has_side_effects=True, vmem_limit_bytes=VMEM_LIMIT),
         )(x, w, scale.reshape(2 * nj, TILE // 2), shift.reshape(2 * nj, TILE // 2))

time: 92.8 us -> 92.5 us (level)
  no operation moved by 1% of the time
where the time goes in v5:
time: 92.5 us; the launch traced here: 92.4 us
  Pallas kernels  90.5 us (98%)
  local copies, waits for them, and re-layouts  1.95 us (2%)
    pallas_call x1, Pallas kernels, local_step(): pl.pallas_call(functools.partial(conv_kernel, half), out_shape=pltpu.VMEM...  90.5 us
    unnamed x1, local copies, waits for them, and re-layouts  1.95 us

profile of v5, /device:TPU:64, one launch (start us, length us, event | category | flops | bytes accessed | tf_op | source)
XLA Modules:
  0.0 92.4 jit_solution(14619693067723924494)
XLA Ops:
  0.0 90.5 %shard_map.46 = bf16[196,8,1280]{2,1,0:T(8,128)(2,1)S(1)} custom-call(bf16[14,14,4,2560]{3,2,1,0:T(4,128)(2,1)} %bitcast.9, bf16[9,1280,2560]{2,1,0:T(8,128)(2,1)} %bitcast.8, f32[10,128]{1,0:T(8,128)} %bitcast.10, f32[10,128]{1,0:T(8,128)} %bitcast.11), custom_call_target="tpu_custom_call" | custom-call | tf_op jit(solution)/shard_map/pallas_call | solution.py:306
  90.5 2.0 %copy.6 = bf16[8,14,14,1280]{3,0,2,1:T(8,128)(2,1)} copy(bf16[8,14,14,1280]{3,0,2,1:T(8,128)(2,1)S(1)} %bitcast.7) | data formatting | bytes 8028160

commit v6 on v5

--- a/solution.py
+++ b/solution.py
@@ -74,7 +74,7 @@
         return z_copy(j, z_rows(s), s)
 
     last_lo, last_hi = OUT_ROWS[1]
-    last_mid = (last_lo + last_hi) // 2
+    last_mid = last_hi - 2
     halves = ((last_lo, last_mid), (last_mid, last_hi))
 
     def z_last(i):

time: 92.5 us -> 92.5 us (level)
  no operation moved by 1% of the time
where the time goes in v6:
time: 92.5 us; the launch traced here: 92.4 us
  Pallas kernels  90.5 us (98%)
  local copies, waits for them, and re-layouts  1.95 us (2%)
    pallas_call x1, Pallas kernels, local_step(): pl.pallas_call(functools.partial(conv_kernel, half), out_shape=pltpu.VMEM...  90.5 us
    unnamed x1, local copies, waits for them, and re-layouts  1.95 us

profile of v6, /device:TPU:64, one launch (start us, length us, event | category | flops | bytes accessed | tf_op | source)
XLA Modules:
  0.0 92.4 jit_solution(18246358079466148062)
XLA Ops:
  0.0 90.5 %shard_map.46 = bf16[196,8,1280]{2,1,0:T(8,128)(2,1)S(1)} custom-call(bf16[14,14,4,2560]{3,2,1,0:T(4,128)(2,1)} %bitcast.9, bf16[9,1280,2560]{2,1,0:T(8,128)(2,1)} %bitcast.8, f32[10,128]{1,0:T(8,128)} %bitcast.10, f32[10,128]{1,0:T(8,128)} %bitcast.11), custom_call_target="tpu_custom_call" | custom-call | tf_op jit(solution)/shard_map/pallas_call | solution.py:306
  90.5 2.0 %copy.6 = bf16[8,14,14,1280]{3,0,2,1:T(8,128)(2,1)} copy(bf16[8,14,14,1280]{3,0,2,1:T(8,128)(2,1)S(1)} %bitcast.7) | data formatting | bytes 8028160

commit v7 on v6

--- a/solution.py
+++ b/solution.py
@@ -58,7 +58,7 @@
 
     def p_send(s, j):
         return pltpu.make_async_remote_copy(
-            src_ref=ps[s].at[j], dst_ref=pr[s].at[j], send_sem=psend.at[s], recv_sem=precv.at[s, j],
+            src_ref=ps[s].at[j], dst_ref=pr[s].at[j], send_sem=psend.at[s], recv_sem=precv.at[lax.rem(s * nj + j, 2)],
             device_id=(pp, peer), device_id_type=MESH)
 
     def z_rows(s):
@@ -260,7 +260,7 @@
 
     for s in range(2):
         pltpu.make_async_remote_copy(
-            src_ref=ps[s], dst_ref=pr[s], send_sem=psend.at[s], recv_sem=precv.at[s, 0],
+            src_ref=ps[s], dst_ref=pr[s], send_sem=psend.at[s], recv_sem=precv.at[0],
             device_id=(pp, peer), device_id_type=MESH).wait_send()
 
     @pl.when(sends_b)
@@ -323,7 +323,7 @@
                 pltpu.VMEM((nj, hh * row, TILE), jnp.bfloat16),
                 pltpu.VMEM((nj, hh * row, TILE), jnp.bfloat16),
                 dma((2,)), dma, pltpu.SemaphoreType.REGULAR, dma((2,)), dma((2,)), dma((2,)), dma((2,)),
-                dma((2,)), dma((2, nj)), dma, dma((4,)),
+                dma((2,)), dma((2,)), dma, dma((4,)),
             ],
             compiler_params=pltpu.CompilerParams(collective_id=0, has_side_effects=True, vmem_limit_bytes=VMEM_LIMIT),
         )(x, w, scale.reshape(2 * nj, TILE // 2), shift.reshape(2 * nj, TILE // 2))

time: 92.5 us -> 92.4 us (level)
  no operation moved by 1% of the time
where the time goes in v7:
time: 92.4 us; the launch traced here: 92.3 us
  Pallas kernels  90.4 us (98%)
  local copies, waits for them, and re-layouts  1.95 us (2%)
    pallas_call x1, Pallas kernels, local_step(): pl.pallas_call(functools.partial(conv_kernel, half), out_shape=pltpu.VMEM...  90.4 us
    unnamed x1, local copies, waits for them, and re-layouts  1.95 us

profile of v7, /device:TPU:64, one launch (start us, length us, event | category | flops | bytes accessed | tf_op | source)
XLA Modules:
  0.0 92.3 jit_solution(1347420109303968353)
XLA Ops:
  0.0 90.4 %shard_map.46 = bf16[196,8,1280]{2,1,0:T(8,128)(2,1)S(1)} custom-call(bf16[14,14,4,2560]{3,2,1,0:T(4,128)(2,1)} %bitcast.9, bf16[9,1280,2560]{2,1,0:T(8,128)(2,1)} %bitcast.8, f32[10,128]{1,0:T(8,128)} %bitcast.10, f32[10,128]{1,0:T(8,128)} %bitcast.11), custom_call_target="tpu_custom_call" | custom-call | tf_op jit(solution)/shard_map/pallas_call | solution.py:306
  90.4 2.0 %copy.6 = bf16[8,14,14,1280]{3,0,2,1:T(8,128)(2,1)} copy(bf16[8,14,14,1280]{3,0,2,1:T(8,128)(2,1)S(1)} %bitcast.7) | data formatting | bytes 8028160
